TPU v7x, 32 devices: a whole 2x2x4 slice. The times are simulated.
32 devices in a mesh: ga: 16 (over z, y, x), band: 2 (over core).
Axes of the slice: x: 2, y: 2, z: 4, core: 2. Of those that a mesh axis runs over, the one named last changes fastest.
Arguments:
- psi: bfloat16 [65536, 2048], P('ga', 'band'), may hold values from -1 to 1
- trial: bfloat16 [65536, 256], P('ga', 'band'), may hold values from -1.25 to 1.25
- beta: bfloat16 [65536, 1536], P('ga'), may hold values from -0.0625 to 0.0625
- q_blocks: float32 [128, 18, 18], replicated, may hold values from -6 to 6
- atom_counts: int32 [128], replicated, may hold values from 1 to 18, 1536 in all
Outputs:
- intersection: float32 [2048, 256], P('band', 'ga')
Inputs may be any that keep to these rules, and one draw needn't show every extreme that they name: `atom_counts`: the counts sum to 1536; atoms own consecutive projectors in order, and some atom has exactly 18.
All inputs are finite; a program needn't handle non-finite values.
Results may differ from a plain program's by a relative error of at most 0.0003.
Values may be sent and summed in bfloat16 or wider, within the bound.
A program may use at most 64 MiB of HBM per device.

v0:
```python
import jax
import jax.numpy as jnp
from jax import lax
from jax.sharding import PartitionSpec as P

MAXP = 18


precise = lax.Precision.HIGHEST


def contract(left, right, precision=None):
    return lax.dot_general(
        left,
        right,
        (((0,), (0,)), ((), ())),
        precision=precision,
        preferred_element_type=jnp.float32,
    )


def locate(ids, offsets):
    below = offsets[None, :] <= ids[:, None]
    atom_ids = jnp.sum(below.astype(jnp.int32), axis=1, dtype=jnp.int32) - 1
    starts = jnp.max(jnp.where(below, offsets[None, :], 0), axis=1)
    return (jnp.clip(atom_ids, 0, offsets.shape[0] - 1), starts)


def atom_window(first, rows, margin, atom_counts, q_blocks, total):
    offsets = jnp.cumsum(atom_counts, dtype=jnp.int32) - atom_counts
    row_ids = first + jnp.arange(rows, dtype=jnp.int32)
    col_ids = first - margin + jnp.arange(rows + 2 * margin, dtype=jnp.int32)
    row_atom, row_start = locate(row_ids, offsets)
    col_atom, col_start = locate(col_ids, offsets)
    inside = (col_ids >= 0) & (col_ids < total)
    same_atom = (row_atom[:, None] == col_atom[None, :]) & inside[None, :]
    extent = q_blocks.shape[1]
    atoms = q_blocks.shape[0]
    row_pos = jnp.clip(row_ids - row_start, 0, extent - 1)
    col_pos = jnp.clip(col_ids - col_start, 0, extent - 1)
    atom_pick = (row_atom[:, None] == jnp.arange(atoms, dtype=jnp.int32)[None, :]).astype(
        jnp.float32
    )
    flat = jnp.dot(
        atom_pick,
        q_blocks.reshape(atoms, extent * extent),
        precision=precise,
        preferred_element_type=jnp.float32,
    )
    flat = flat.reshape(rows, extent, extent)
    row_pick = (row_pos[:, None] == jnp.arange(extent, dtype=jnp.int32)[None, :]).astype(
        jnp.float32
    )
    q_rows = jnp.sum(flat * row_pick[:, :, None], axis=1)
    col_pick = (jnp.arange(extent, dtype=jnp.int32)[:, None] == col_pos[None, :]).astype(
        jnp.float32
    )
    entries = jnp.dot(q_rows, col_pick, precision=precise, preferred_element_type=jnp.float32)
    return jnp.where(same_atom, entries, jnp.zeros_like(entries))


def apply_blocks(block_rows, atom_counts, q_blocks, margin):
    total = block_rows.shape[0]
    tile = 128
    padded = jnp.pad(block_rows, ((margin, margin), (0, 0)))

    def one_tile(first):
        window = atom_window(first, tile, margin, atom_counts, q_blocks, total)
        rows = lax.dynamic_slice_in_dim(padded, first, tile + 2 * margin, 0)
        return jnp.dot(window, rows, precision=precise, preferred_element_type=jnp.float32)

    starts = jnp.arange(total // tile, dtype=jnp.int32) * tile
    return lax.map(one_tile, starts).reshape(total, block_rows.shape[1])


def shards(psi, trial, beta, q_blocks, atom_counts):
    trial_full = lax.all_gather(trial, "band", axis=1, tiled=True)
    plain = contract(psi, trial_full)
    own_trial = lax.psum(contract(beta, trial), "ga")
    weighted = apply_blocks(own_trial, atom_counts, q_blocks, MAXP)
    lifted = jnp.dot(
        beta.astype(jnp.float32), weighted, precision=precise, preferred_element_type=jnp.float32
    )
    lifted_full = lax.all_gather(lifted, "band", axis=1, tiled=True)
    augment = contract(psi.astype(jnp.float32), lifted_full, precise)
    return lax.psum_scatter(plain + augment, "ga", scatter_dimension=1, tiled=True)


def solution(mesh):
    in_specs = (P("ga", "band"), P("ga", "band"), P("ga", None), P(), P())
    out_specs = P("band", "ga")
    return jax.shard_map(shards, mesh=mesh, in_specs=in_specs, out_specs=out_specs, check_vma=False)
```

profile of v0, /device:TPU:0, one launch (start us, length us, event | category | flops | bytes accessed | tf_op | source)
XLA Modules:
  0.0 336.6 jit_solution(15740156071846685891)
XLA Ops:
  7.4 9.2 %fusion.15 = f32[1536,128]{1,0:T(8,128)} fusion(bf16[4096,1536]{1,0:T(8,128)(2,1)} %param.9, bf16[4096,128]{1,0:T(8,128)(2,1)} %param.8), kind=kOutput, calls=%fused_computation.35 | convolution fusion | flops 1610612736 | bytes 14417920 | tf_op jit(solution)/shard_map/dot_general | solution.py:13
  16.7 0.5 all-gather.3.cloned.1.call-update
  17.7 112.6 %all-reduce.3.cloned.1.call-done = f32[1536,128]{1,0:T(8,128)} async-done(((f32[1536,128]{1,0:T(8,128)}), f32[1536,128]{1,0:T(8,128)}) %all-reduce.3.cloned.1.call-update) | async-done | bytes 786448 | tf_op jit(solution)/shard_map/psum | solution.py:79
  130.3 1.2 pad.4
  131.5 76.7 %while.14 = (s32[]{:T(128)}, f32[12,128,128]{2,1,0:T(8,128)S(1)}, s32[1,128]{1,0:T(1,128)S(1)}, s32[12]{0:T(128)S(1)}, f32[128,18,18]{0,2,1:T(8,128)}, /*index=5...) while((s32[]{:T(128)}, f32[12,128,128]{2,1,0:T(8,128)S(1)}, ...), condition=%wide.wide.region_8.9_spmd, body=%wide.wide.region_2.8_spmd.sunk | while | flops 100835240 | bytes 869803 | solution.py:73
  131.5 0.7 dynamic_slice.22
  132.2 0.7 iota_add_fusion.6
  133.0 0.7 subtract_clamp_fusion.6
  137.9 0.7 dynamic_slice.22
  138.6 0.7 iota_add_fusion.6
  139.4 0.7 subtract_clamp_fusion.6
  143.8 0.4 fusion.56
  144.3 0.7 dynamic_slice.22
  145.0 0.7 iota_add_fusion.6
  145.8 0.7 subtract_clamp_fusion.6
  150.7 0.7 dynamic_slice.22
  151.3 0.7 iota_add_fusion.6
  152.2 0.7 subtract_clamp_fusion.6
  156.6 0.4 fusion.56
  157.1 0.7 dynamic_slice.22
  157.7 0.7 iota_add_fusion.6
  158.6 0.7 subtract_clamp_fusion.6
  163.5 0.7 dynamic_slice.22
  164.1 0.7 iota_add_fusion.6
  165.0 0.7 subtract_clamp_fusion.6
  169.9 0.7 dynamic_slice.22
  170.5 0.7 iota_add_fusion.6
  171.4 0.7 subtract_clamp_fusion.6
  176.2 0.7 dynamic_slice.22
  176.9 0.7 iota_add_fusion.6
  177.8 0.7 subtract_clamp_fusion.6
  182.6 0.7 dynamic_slice.22
  183.3 0.7 iota_add_fusion.6
  184.2 0.7 subtract_clamp_fusion.6
  189.0 0.7 dynamic_slice.22
  189.7 0.7 iota_add_fusion.6
  190.6 0.7 subtract_clamp_fusion.6
  195.4 0.7 dynamic_slice.22
  196.1 0.7 iota_add_fusion.6
  197.0 0.7 subtract_clamp_fusion.6
  201.8 0.7 dynamic_slice.22
  202.5 0.7 iota_add_fusion.6
  203.4 0.7 subtract_clamp_fusion.6
  208.2 17.0 %convolution_bitcast_fusion.1 = f32[4096,128]{0,1:T(8,128)} fusion(f32[1536,128]{1,0:T(8,128)S(1)} %bitcast.58, bf16[4096,1536]{1,0:T(8,128)(2,1)} %param.9), kind=kOutput, calls=%fused_computation.29 | convolution fusion | flops 9663676416 | bytes 15466496 | tf_op jit(solution)/shard_map/dot_general | solution.py:81
  225.5 6.3 %fusion.14 = f32[1024,256]{0,1:T(8,128)S(1)} fusion(bf16[4096,1024]{1,0:T(8,128)(2,1)} %param.7, bf16[4096,256]{1,0:T(8,128)(2,1)} %all-gather.3.cloned.1.call-done), kind=kOutput, calls=%fused_computation.34 | convolution fusion | flops 2147483648 | bytes 11534336 | tf_op jit(solution)/shard_map/dot_general | solution.py:13
  231.9 6.3 %all-gather.5.cloned.1.call-done = f32[4096,256]{0,1:T(8,128)} async-done(((f32[4096,128]{0,1:T(8,128)}), f32[4096,256]{0,1:T(8,128)}) %all-gather.5.cloned.1.call-update) | async-done | bytes 4194320 | tf_op jit(solution)/shard_map/all_gather | solution.py:84
  238.2 11.1 %fusion.13 = f32[1024,256]{0,1:T(8,128)} fusion(f32[1024,256]{0,1:T(8,128)S(1)} %fusion.14, f32[4096,256]{0,1:T(8,128)} %all-gather.5.cloned.1.call-done, bf16[4096,1024]{1,0:T(8,128)(2,1)} %param.7), kind=kOutput, calls=%fused_computation.31 | convolution fusion | flops 12885164032 | bytes 14680064 | tf_op jit(solution)/shard_map/dot_general | solution.py:13
  249.3 79.9 %reduce-scatter.2.cloned.1.call-done = f32[1024,16]{0,1:T(8,128)} async-done(((f32[1024,256]{0,1:T(8,128)}), f32[1024,16]{0,1:T(8,128)}) %reduce-scatter.2.cloned.1.call-update) | async-done | bytes 65552 | tf_op jit(solution)/shard_map/reduce_scatter | solution.py:86
  (137 shorter events, 17.7 us)
Async XLA Ops:
  7.4 9.9 %copy-start = (f32[128,18,18]{0,2,1:T(8,128)S(1)}, f32[128,18,18]{0,2,1:T(8,128)}, u32[]{:S(2)}) copy-start(f32[128,18,18]{0,2,1:T(8,128)} %param.10) | copy-start | bytes 497668
  7.4 9.9 %copy-start.1 = (s32[128]{0:T(128)S(1)}, s32[128]{0:T(128)}, u32[]{:S(2)}) copy-start(s32[128]{0:T(128)} %param.11) | copy-start | bytes 1540
  7.4 122.9 %all-reduce.3.cloned.1.call-start = ((), (), s32[]{:S(2)}) async-start(), calls=%async_computation.2 | async-start | bytes 1572864 | tf_op jit(solution)/shard_map/psum | solution.py:79
  16.6 208.9 %all-gather.3.cloned.1.call-start = ((), (), s32[]{:S(2)}) async-start(), calls=%async_computation.1 | async-start | bytes 3145728 | tf_op jit(solution)/shard_map/all_gather | solution.py:77
  17.2 220.9 %all-gather.5.cloned.1.call-start = ((), (), s32[]{:S(2)}) async-start(), calls=%async_computation.3 | async-start | bytes 6291456 | tf_op jit(solution)/shard_map/all_gather | solution.py:84
  225.3 103.9 %reduce-scatter.2.cloned.1.call-start = ((), (), s32[]{:S(2)}) async-start(), calls=%async_computation.4 | async-start | bytes 1114112 | tf_op jit(solution)/shard_map/reduce_scatter | solution.py:86
Sparse Core Ops, SparseCore 0:
  16.7 113.5 all-reduce.2
  249.4 79.7 reduce-scatter.1
Sparse Core Ops, SparseCore 1:
  18.6 12.7 all-gather.2
  225.3 12.8 all-gather.4
where the time goes:
time: 338 us; the launch traced here: 337 us
  waiting for transfers between devices  199 us (59%)
  matrix products  56.3 us (17%)
  loops' own time  34.2 us (10%)
  other arithmetic  22 us (7%)
  between operations  14.9 us (4%)
  local copies, waits for them, and re-layouts  9.52 us (3%)
    psum x1, waiting for transfers between devices, shards(): own_trial = lax.psum(contract(beta, trial), 'ga')  113 us
    reduce_scatter x1, waiting for transfers between devices, shards(): lax.psum_scatter(plain + augment, 'ga', scatter_dimension=1, tiled=True)  79.9 us
    another operation x1, loops' own time, apply_blocks(): return lax.map(one_tile, starts).reshape(total, block_rows.shape[1])  34.2 us
    dot_general x3, matrix products, contract(): lax.dot_general(left, right, (((0,), (0,)), ((), ())), precision=precisio...  26.7 us
    dot_general x1, matrix products, shards(): jnp.dot(beta.astype(jnp.float32), weighted, precision=precise, preferred_...  17 us
    min x12, other arithmetic, atom_window(): row_pos = jnp.clip(row_ids - row_start, 0, extent - 1)  8.38 us
    add x12, other arithmetic, atom_window(): row_ids = first + jnp.arange(rows, dtype=jnp.int32)  8.29 us
    dynamic_slice x12, local copies, waits for them, and re-layouts, apply_blocks(): return lax.map(one_tile, starts).reshape(total, block_rows.shape[1])  8 us
  transfers between devices with their start and end apart: 4, of which 3 were waited for; matrix products, arithmetic and copies ran while one was open for 20% of the time, Pallas kernels for 0%

commit v1 on v0

v1 whole, which is shorter than its diff:
```python
import functools

import jax
import jax.numpy as jnp
from jax import lax
from jax.experimental import pallas as pl
from jax.experimental.pallas import tpu as pltpu
from jax.sharding import PartitionSpec as P

MESH = pl.DeviceIdType.MESH
precise = lax.Precision.HIGHEST
F32, BF16 = jnp.float32, jnp.bfloat16


def contract(left, right, precision=None):
    return lax.dot_general(
        left, right, (((0,), (0,)), ((), ())), precision=precision, preferred_element_type=F32
    )


def split2(x):
    hi = x.astype(BF16)
    return hi, (x - hi.astype(F32)).astype(BF16)


def kernel(
    n, maxp, psi_h, trial_h, beta_h, q_ref, cnt_ref, out_ref,
    psi_v, beta_v, trial_v, trial_t, q_parts, qd, proj, rs1, wall, whl, s_buf, fin, rs2,
    trial_sem, beta_sem, psi_sem, send1, recv1, send2, recv2, xs, xr, send3, recv3,
):
    me = lax.axis_index("ga")
    band = lax.axis_index("band")
    g, cols = trial_v.shape
    p_size = beta_v.shape[1]
    nbands = psi_v.shape[1]
    natom = cnt_ref.shape[1]
    mp = q_ref.shape[0] // maxp
    r1 = cols // n
    r2 = out_ref.shape[0]
    beta_chunks = beta_sem.shape[0]
    bw = p_size // beta_chunks
    psi_chunks = psi_sem.shape[0]
    pw = nbands // psi_chunks
    s_chunks = xs.shape[0]
    sw = g // s_chunks

    def aligned(i, size):
        return pl.ds(pl.multiple_of(i * size, size), size)

    def beta_copy(c):
        at = (slice(None), pl.ds(c * bw, bw))
        return pltpu.make_async_copy(beta_h.at[at], beta_v.at[at], beta_sem.at[c])

    def psi_copy(c):
        at = (slice(None), pl.ds(c * pw, pw))
        return pltpu.make_async_copy(psi_h.at[at], psi_v.at[at], psi_sem.at[c])

    trial_copy = pltpu.make_async_copy(trial_h, trial_v, trial_sem)
    trial_copy.start()
    for c in range(beta_chunks):
        beta_copy(c).start()
    for c in range(psi_chunks):
        psi_copy(c).start()

    barrier = pltpu.get_barrier_semaphore()

    def greet(d, _):
        pl.semaphore_signal(
            barrier, inc=1, device_id=(lax.rem(me + d, n), band), device_id_type=MESH
        )
        return 0

    lax.fori_loop(1, n, greet, 0)
    pl.semaphore_signal(barrier, inc=1, device_id=(me, 1 - band), device_id_type=MESH)

    cnt = cnt_ref[...].astype(F32)
    row = lax.broadcasted_iota(jnp.int32, (natom, natom), 0)
    col = lax.broadcasted_iota(jnp.int32, (natom, natom), 1)
    offs = jnp.sum(jnp.where(col < row, cnt, 0.0), axis=1, keepdims=True)
    own = jnp.sum(jnp.where(col == row, cnt, 0.0), axis=1, keepdims=True)
    q = q_ref[...]
    q_hi = q.astype(BF16)
    rest = q - q_hi.astype(F32)
    q_mid = rest.astype(BF16)
    q_parts[0] = q_hi
    q_parts[1] = q_mid
    q_parts[2] = (rest - q_mid.astype(F32)).astype(BF16)
    lanes = 256
    nd = qd.shape[0]

    def diagonals(c, _):
        ids = (c * lanes + lax.broadcasted_iota(jnp.int32, (natom, lanes), 1)).astype(F32)
        owns = (offs <= ids) & (ids < offs + own)
        pos = jnp.sum(jnp.where(owns, ids - offs, 0.0), axis=0, keepdims=True)
        count = jnp.sum(jnp.where(owns, jnp.broadcast_to(own, owns.shape), 0.0), axis=0, keepdims=True)
        pick = jnp.where(owns, 1.0, 0.0).astype(BF16)
        flat = jnp.dot(q_parts[0], pick, preferred_element_type=F32)
        flat += jnp.dot(q_parts[1], pick, preferred_element_type=F32)
        flat += jnp.dot(q_parts[2], pick, preferred_element_type=F32)
        q_row = jnp.zeros((mp, lanes), F32)
        for i in range(maxp):
            q_row += jnp.where(pos == float(i), flat[i * mp : (i + 1) * mp], 0.0)
        at = pos + lax.broadcasted_iota(jnp.int32, (nd, lanes), 0).astype(F32) - float(maxp - 1)
        entries = jnp.zeros((nd, lanes), F32)
        for j in range(maxp):
            entries += jnp.where(at == float(j), q_row[j : j + 1], 0.0)
        qd[:, aligned(c, lanes)] = jnp.where(at < count, entries, 0.0)
        return 0

    lax.fori_loop(0, p_size // lanes, diagonals, 0)

    trial_copy.wait()

    def turn(k, _):
        trial_t[:, aligned(k, sw)] = trial_v[aligned(k, sw), :].T
        return 0

    lax.fori_loop(0, s_chunks, turn, 0)

    pl.semaphore_wait(barrier, n)

    def scatter1(c, d):
        peer = lax.rem(me + d, n)
        at = pl.ds(c * bw, bw)
        return pltpu.make_async_remote_copy(
            src_ref=proj.at[aligned(peer, r1), at],
            dst_ref=rs1.at[d, :, at],
            send_sem=send1.at[c, d],
            recv_sem=recv1.at[c, d],
            device_id=(peer, band),
            device_id_type=MESH,
        )

    for c in range(beta_chunks):
        beta_copy(c).wait()
        at = pl.ds(c * bw, bw)
        proj[:, at] = jnp.dot(trial_t[...], beta_v[:, at], preferred_element_type=F32)

        def start1(d, _, c=c):
            scatter1(c, d).start()
            return 0

        lax.fori_loop(1, n, start1, 0)

    for c in range(beta_chunks):

        def wait1(d, _, c=c):
            scatter1(c, d).wait()
            return 0

        lax.fori_loop(1, n, wait1, 0)

    def add1(d, total):
        return total + rs1[d]

    x = lax.fori_loop(1, n, add1, proj[aligned(me, r1), :])
    acc = jnp.zeros_like(x)
    for d in range(2 * maxp - 1):
        shift = (maxp - 1 - d) % p_size
        moved = x if shift == 0 else pltpu.roll(x, shift, axis=1)
        acc += qd[d : d + 1, :] * moved
    wall[aligned(me, r1), :] = acc

    def gather(d):
        peer = lax.rem(me + d, n)
        return pltpu.make_async_remote_copy(
            src_ref=wall.at[aligned(me, r1), :],
            dst_ref=wall.at[aligned(me, r1), :],
            send_sem=send2.at[d],
            recv_sem=recv2.at[d],
            device_id=(peer, band),
            device_id_type=MESH,
        )

    def start2(d, _):
        gather(d).start()
        return 0

    def wait2(d, _):
        gather(d).wait()
        return 0

    lax.fori_loop(1, n, start2, 0)
    lax.fori_loop(1, n, wait2, 0)
    hi, lo = split2(wall[...])
    whl[:cols, :] = hi
    whl[cols:, :] = lo

    base = band * (2 * cols)

    def exchange(k):
        at = (pl.ds(pl.multiple_of(base, 2 * cols), 2 * cols), aligned(k, sw))
        return pltpu.make_async_remote_copy(
            src_ref=s_buf.at[at],
            dst_ref=s_buf.at[at],
            send_sem=xs.at[k],
            recv_sem=xr.at[k],
            device_id=(me, 1 - band),
            device_id_type=MESH,
        )

    def lift(k, _):
        both = lax.dot_general(
            whl[...], beta_v[aligned(k, sw), :], (((1,), (1,)), ((), ())), preferred_element_type=F32
        )
        s = both[:cols] + both[cols:] + trial_t[:, aligned(k, sw)].astype(F32)
        s_hi, s_lo = split2(s)
        s_buf[pl.ds(pl.multiple_of(base, 2 * cols), cols), aligned(k, sw)] = s_hi
        s_buf[pl.ds(pl.multiple_of(base + cols, cols), cols), aligned(k, sw)] = s_lo
        exchange(k).start()
        return 0

    lax.fori_loop(0, s_chunks, lift, 0)

    def wait_x(k, _):
        exchange(k).wait()
        return 0

    lax.fori_loop(0, s_chunks, wait_x, 0)

    def scatter3(c, d):
        peer = lax.rem(me + d, n)
        return pltpu.make_async_remote_copy(
            src_ref=fin.at[aligned(peer, r2), aligned(c, pw)],
            dst_ref=rs2.at[d, :, aligned(c, pw)],
            send_sem=send3.at[c, d],
            recv_sem=recv3.at[c, d],
            device_id=(peer, band),
            device_id_type=MESH,
        )

    for c in range(psi_chunks):
        psi_copy(c).wait()

    def share(c, _):
        f = jnp.dot(s_buf[...], psi_v[:, aligned(c, pw)], preferred_element_type=F32)
        for b in range(2):
            at = 2 * b * cols
            fin[b * cols : (b + 1) * cols, aligned(c, pw)] = (
                f[at : at + cols] + f[at + cols : at + 2 * cols]
            )

        def start3(d, _):
            scatter3(c, d).start()
            return 0

        lax.fori_loop(1, n, start3, 0)
        return 0

    lax.fori_loop(0, psi_chunks, share, 0)

    def finish(c, _):
        def wait3(d, total):
            scatter3(c, d).wait()
            return total + rs2[d, :, aligned(c, pw)]

        out_ref[:, aligned(c, pw)] = lax.fori_loop(
            1, n, wait3, fin[aligned(me, r2), aligned(c, pw)]
        )
        return 0

    lax.fori_loop(0, psi_chunks, finish, 0)


def fused(n, blk, psi, trial, beta, q_blocks, atom_counts):
    g, cols = trial.shape
    nbands = psi.shape[1]
    p_size = beta.shape[1]
    natom, maxp = q_blocks.shape[:2]
    mp = -(-maxp // 8) * 8
    nd = -(-(2 * maxp - 1) // 8) * 8
    r1, r2 = cols // n, blk // n
    beta_chunks, psi_chunks, s_chunks = 3, 4, 8
    q_flat = jnp.pad(q_blocks, ((0, 0), (0, 0), (0, mp - maxp)))
    q_flat = q_flat.transpose(1, 2, 0).reshape(maxp * mp, natom)
    dma = pltpu.SemaphoreType.DMA
    out = pl.pallas_call(
        functools.partial(kernel, n, maxp),
        out_shape=jax.ShapeDtypeStruct((r2, nbands), F32),
        in_specs=[pl.BlockSpec(memory_space=pl.ANY)] * 3
        + [pl.BlockSpec(memory_space=pltpu.VMEM)] * 2,
        out_specs=pl.BlockSpec(memory_space=pltpu.VMEM),
        scratch_shapes=[
            pltpu.VMEM((g, nbands), BF16),
            pltpu.VMEM((g, p_size), BF16),
            pltpu.VMEM((g, cols), BF16),
            pltpu.VMEM((cols, g), BF16),
            pltpu.VMEM((3, maxp * mp, natom), BF16),
            pltpu.VMEM((nd, p_size), F32),
            pltpu.VMEM((cols, p_size), F32),
            pltpu.VMEM((n, r1, p_size), F32),
            pltpu.VMEM((cols, p_size), F32),
            pltpu.VMEM((2 * cols, p_size), BF16),
            pltpu.VMEM((4 * cols, g), BF16),
            pltpu.VMEM((2 * cols, nbands), F32),
            pltpu.VMEM((n, r2, nbands), F32),
            dma,
            dma((beta_chunks,)),
            dma((psi_chunks,)),
            dma((beta_chunks, n)),
            dma((beta_chunks, n)),
            dma((n,)),
            dma((n,)),
            dma((s_chunks,)),
            dma((s_chunks,)),
            dma((psi_chunks, n)),
            dma((psi_chunks, n)),
        ],
        compiler_params=pltpu.CompilerParams(
            collective_id=0, has_side_effects=True, vmem_limit_bytes=60 * 1024 * 1024
        ),
    )(psi, trial, beta, q_flat, atom_counts.reshape(1, natom))
    return out.T


def q_dense(atom_counts, q_blocks, p_size):
    offsets = jnp.cumsum(atom_counts, dtype=jnp.int32) - atom_counts
    natom, maxp = q_blocks.shape[:2]
    ids = jnp.arange(p_size, dtype=jnp.int32)
    owns = (offsets[None, :] <= ids[:, None]) & (ids[:, None] < (offsets + atom_counts)[None, :])
    pos = jnp.sum(jnp.where(owns, ids[:, None] - offsets[None, :], 0), axis=1)
    atom = jnp.sum(jnp.where(owns, jnp.arange(natom, dtype=jnp.int32)[None, :], 0), axis=1)
    flat = jnp.dot(owns.astype(F32), q_blocks.reshape(natom, maxp * maxp), precision=precise)
    place = pos[:, None] == jnp.arange(maxp, dtype=jnp.int32)[None, :]
    rows = jnp.sum(jnp.where(place[:, :, None], flat.reshape(p_size, maxp, maxp), 0.0), axis=1)
    entries = jnp.dot(rows, place.astype(F32).T, precision=precise)
    return jnp.where(atom[:, None] == atom[None, :], entries, 0.0)


def general(psi, trial, beta, q_blocks, atom_counts):
    own = lax.psum(contract(beta, trial), "ga")
    weighted = jnp.dot(q_dense(atom_counts, q_blocks, beta.shape[1]), own, precision=precise)
    w_hi, w_lo = split2(weighted)
    both = jnp.dot(beta, jnp.concatenate([w_hi, w_lo], axis=1), preferred_element_type=F32)
    cols = trial.shape[1]
    s = both[:, :cols] + both[:, cols:] + trial.astype(F32)
    s_hi, s_lo = split2(lax.all_gather(s, "band", axis=1, tiled=True))
    part = contract(psi, s_hi) + contract(psi, s_lo)
    return lax.psum_scatter(part, "ga", scatter_dimension=1, tiled=True)


def solution(mesh):
    n, bands = mesh.shape["ga"], mesh.shape["band"]

    def shards(psi, trial, beta, q_blocks, atom_counts):
        g, cols = trial.shape
        blk = cols * bands
        fits = (
            bands == 2
            and cols % 128 == 0
            and cols % (8 * n) == 0
            and blk % (8 * n) == 0
            and g % 4096 == 0
            and beta.shape[1] % 768 == 0
            and psi.shape[1] % 512 == 0
            and q_blocks.shape[0] % 128 == 0
        )
        if fits:
            return fused(n, blk, psi, trial, beta, q_blocks, atom_counts)
        return general(psi, trial, beta, q_blocks, atom_counts)

    in_specs = (P("ga", "band"), P("ga", "band"), P("ga", None), P(), P())
    out_specs = P("band", "ga")
    return jax.shard_map(shards, mesh=mesh, in_specs=in_specs, out_specs=out_specs, check_vma=False)
```

time: 338 us -> 84.8 us (0.25)
  waiting for transfers between devices: 199 us -> 0 us
  Pallas kernels: 0 us -> 81.5 us
  matrix products: 56.3 us -> 0 us
  loops' own time: 34.2 us -> 0 us
  other arithmetic: 22 us -> 0 us
  between operations: 14.9 us -> 0.01 us
  local copies, waits for them, and re-layouts: 9.52 us -> 3.1 us
    psum x1 -> x0, waiting for transfers between devices: 113 us -> none  [shards(): own_trial = lax.psum(contract(beta, trial), 'ga')]
    pallas_call x0 -> x1, Pallas kernels: none -> 81.5 us  [fused(): pl.pallas_call(functools.partial(kernel, n, maxp), out_shape=jax.ShapeDty...]
    reduce_scatter x1 -> x0, waiting for transfers between devices: 79.9 us -> none  [shards(): lax.psum_scatter(plain + augment, 'ga', scatter_dimension=1, tiled=True)]
    dot_general x40 -> x0, matrix products: 56.3 us -> none  [the longest x3 26.7 us: contract(): lax.dot_general(left, right, (((0,), (0,)), ((), ())), precision=precisio...]
    another operation x1 -> x0, loops' own time: 34.2 us -> none  [apply_blocks(): return lax.map(one_tile, starts).reshape(total, block_rows.shape[1])]
    min x24 -> x0, other arithmetic: 8.49 us -> none  [the longest x12 8.38 us: atom_window(): row_pos = jnp.clip(row_ids - row_start, 0, extent - 1)]
    add x24 -> x0, other arithmetic: 8.33 us -> none  [the longest x12 8.29 us: atom_window(): row_ids = first + jnp.arange(rows, dtype=jnp.int32)]
    dynamic_slice x12 -> x0, local copies, waits for them, and re-layouts: 8 us -> none  [apply_blocks(): return lax.map(one_tile, starts).reshape(total, block_rows.shape[1])]
  transfers between devices with their start and end apart: 4 -> 0, of which waited for: 3 -> 0; matrix products, arithmetic and copies ran while one was open for 20% -> 0% of each run, Pallas kernels for 0% -> 0%
where the time goes in v1:
time: 84.8 us; the launch traced here: 84.6 us
  Pallas kernels  81.5 us (96%)
  local copies, waits for them, and re-layouts  3.1 us (4%)
    pallas_call x1, Pallas kernels, fused(): pl.pallas_call(functools.partial(kernel, n, maxp), out_shape=jax.ShapeDty...  81.5 us

profile of v1, /device:TPU:0, one launch (start us, length us, event | category | flops | bytes accessed | tf_op | source)
XLA Modules:
  0.0 84.6 jit_solution(2380127781793521475)
XLA Ops:
  0.0 1.6 %pad.4 = f32[128,18,24]{0,2,1:T(8,128)} pad(f32[128,18,18]{0,2,1:T(8,128)} %param.8, f32[]{:T(128)} %constant.2.clone.1), padding=0_0x0_0x0_6 | pad | bytes 387076 | tf_op jit(solution)/shard_map/jit(_pad)/pad | solution.py:274
  1.6 81.5 %shard_map.55 = f32[16,1024]{1,0:T(8,128)} custom-call(bf16[4096,1024]{1,0:T(8,128)(2,1)} %psi_h.1, bf16[4096,128]{1,0:T(8,128)(2,1)} %trial_h.1, bf16[4096,1536]{1,0:T(8,128)(2,1)} %beta_h.1, f32[432,128]{1,0:T(8,128)} %bitcast.5, s32[1,128]{1,0:T(1,128)} %bitcast.7), custom_call_target="tpu_custom_call" | custom-call | tf_op jit(solution)/shard_map/pallas_call | solution.py:277
  83.1 1.5 %copy.7 = f32[1024,16]{0,1:T(8,128)} copy(f32[1024,16]{0,1:T(8,128)} %bitcast.6) | data formatting | bytes 131072

commit v2 on v1

--- a/solution.py
+++ b/solution.py
@@ -24,12 +24,25 @@
 
 
 def kernel(
-    n, maxp, psi_h, trial_h, beta_h, q_ref, cnt_ref, out_ref,
-    psi_v, beta_v, trial_v, trial_t, q_parts, qd, proj, rs1, wall, whl, s_buf, fin, rs2,
-    trial_sem, beta_sem, psi_sem, send1, recv1, send2, recv2, xs, xr, send3, recv3,
+    n, inner, maxp, psi_h, trial_h, beta_h, q_ref, cnt_ref, out_ref,
+    psi_v, beta_v, trial_v, trial_t, q_parts, qd, proj, in1, mid1, end1, wall, whl, s_buf,
+    fin, in3, mid3, end3, trial_sem, beta_sem, psi_sem, send1, recv1, send1b, recv1b,
+    send2, recv2, send2b, recv2b, xs, xr, send3, recv3, send3b, recv3b,
 ):
     me = lax.axis_index("ga")
     band = lax.axis_index("band")
+    outer = n // inner
+    w, z = lax.rem(me, inner), lax.div(me, inner)
+
+    def mate(d):
+        return lax.rem(w + d, inner)
+
+    def far(e):
+        return lax.rem(z + e, outer)
+
+    def reach(to_z, to_w):
+        return dict(device_id=(to_z * inner + to_w, band), device_id_type=MESH)
+
     g, cols = trial_v.shape
     p_size = beta_v.shape[1]
     nbands = psi_v.shape[1]
@@ -45,7 +58,7 @@
     sw = g // s_chunks
 
     def aligned(i, size):
-        return pl.ds(pl.multiple_of(i * size, size), size)
+        return pl.ds(i * size if isinstance(i, int) else pl.multiple_of(i * size, size), size)
 
     def beta_copy(c):
         at = (slice(None), pl.ds(c * bw, bw))
@@ -64,13 +77,10 @@
 
     barrier = pltpu.get_barrier_semaphore()
 
-    def greet(d, _):
-        pl.semaphore_signal(
-            barrier, inc=1, device_id=(lax.rem(me + d, n), band), device_id_type=MESH
-        )
-        return 0
-
-    lax.fori_loop(1, n, greet, 0)
+    for d in range(1, inner):
+        pl.semaphore_signal(barrier, inc=1, **reach(z, mate(d)))
+    for e in range(1, outer):
+        pl.semaphore_signal(barrier, inc=1, **reach(far(e), w))
     pl.semaphore_signal(barrier, inc=1, device_id=(me, 1 - band), device_id_type=MESH)
 
     cnt = cnt_ref[...].astype(F32)
@@ -117,71 +127,91 @@
 
     lax.fori_loop(0, s_chunks, turn, 0)
 
-    pl.semaphore_wait(barrier, n)
-
-    def scatter1(c, d):
-        peer = lax.rem(me + d, n)
+    pl.semaphore_wait(barrier, inner + outer - 1)
+
+    def inner1(c, d):
         at = pl.ds(c * bw, bw)
         return pltpu.make_async_remote_copy(
-            src_ref=proj.at[aligned(peer, r1), at],
-            dst_ref=rs1.at[d, :, at],
+            src_ref=proj.at[aligned(mate(d), outer * r1), at],
+            dst_ref=in1.at[d, :, at],
             send_sem=send1.at[c, d],
             recv_sem=recv1.at[c, d],
-            device_id=(peer, band),
-            device_id_type=MESH,
-        )
+            **reach(z, mate(d)),
+        )
+
+    def outer1(c, e):
+        at = pl.ds(c * bw, bw)
+        return pltpu.make_async_remote_copy(
+            src_ref=mid1.at[aligned(far(e), r1), at],
+            dst_ref=end1.at[e, :, at],
+            send_sem=send1b.at[c, e],
+            recv_sem=recv1b.at[c, e],
+            **reach(far(e), w),
+        )
+
+    def middle1(c):
+        at = pl.ds(c * bw, bw)
+        total = proj[aligned(w, outer * r1), at]
+        for d in range(1, inner):
+            inner1(c, d).wait()
+            total += in1[d, :, at]
+        mid1[:, at] = total
+        for e in range(1, outer):
+            outer1(c, e).start()
 
     for c in range(beta_chunks):
         beta_copy(c).wait()
         at = pl.ds(c * bw, bw)
         proj[:, at] = jnp.dot(trial_t[...], beta_v[:, at], preferred_element_type=F32)
-
-        def start1(d, _, c=c):
-            scatter1(c, d).start()
-            return 0
-
-        lax.fori_loop(1, n, start1, 0)
+        for d in range(1, inner):
+            inner1(c, d).start()
+        if c:
+            middle1(c - 1)
+    middle1(beta_chunks - 1)
 
     for c in range(beta_chunks):
-
-        def wait1(d, _, c=c):
-            scatter1(c, d).wait()
-            return 0
-
-        lax.fori_loop(1, n, wait1, 0)
-
-    def add1(d, total):
-        return total + rs1[d]
-
-    x = lax.fori_loop(1, n, add1, proj[aligned(me, r1), :])
+        for e in range(1, outer):
+            outer1(c, e).wait()
+    x = mid1[aligned(z, r1), :]
+    for e in range(1, outer):
+        x += end1[e]
     acc = jnp.zeros_like(x)
     for d in range(2 * maxp - 1):
         shift = (maxp - 1 - d) % p_size
         moved = x if shift == 0 else pltpu.roll(x, shift, axis=1)
         acc += qd[d : d + 1, :] * moved
-    wall[aligned(me, r1), :] = acc
-
-    def gather(d):
-        peer = lax.rem(me + d, n)
-        return pltpu.make_async_remote_copy(
-            src_ref=wall.at[aligned(me, r1), :],
-            dst_ref=wall.at[aligned(me, r1), :],
-            send_sem=send2.at[d],
-            recv_sem=recv2.at[d],
-            device_id=(peer, band),
-            device_id_type=MESH,
-        )
-
-    def start2(d, _):
-        gather(d).start()
-        return 0
-
-    def wait2(d, _):
-        gather(d).wait()
-        return 0
-
-    lax.fori_loop(1, n, start2, 0)
-    lax.fori_loop(1, n, wait2, 0)
+    mine = w * outer + z
+    wall[aligned(mine, r1), :] = acc
+
+    def outer2(e):
+        return pltpu.make_async_remote_copy(
+            src_ref=wall.at[aligned(mine, r1), :],
+            dst_ref=wall.at[aligned(mine, r1), :],
+            send_sem=send2.at[e],
+            recv_sem=recv2.at[e],
+            **reach(far(e), w),
+        )
+
+    def inner2(e, d):
+        block = w * outer + lax.rem(z + outer - e, outer)
+        return pltpu.make_async_remote_copy(
+            src_ref=wall.at[aligned(block, r1), :],
+            dst_ref=wall.at[aligned(block, r1), :],
+            send_sem=send2b.at[e, d],
+            recv_sem=recv2b.at[e, d],
+            **reach(z, mate(d)),
+        )
+
+    for e in range(1, outer):
+        outer2(e).start()
+    for e in range(outer):
+        if e:
+            outer2(e).wait()
+        for d in range(1, inner):
+            inner2(e, d).start()
+    for e in range(outer):
+        for d in range(1, inner):
+            inner2(e, d).wait()
     hi, lo = split2(wall[...])
     whl[:cols, :] = hi
     whl[cols:, :] = lo
@@ -218,51 +248,65 @@
 
     lax.fori_loop(0, s_chunks, wait_x, 0)
 
-    def scatter3(c, d):
-        peer = lax.rem(me + d, n)
-        return pltpu.make_async_remote_copy(
-            src_ref=fin.at[aligned(peer, r2), aligned(c, pw)],
-            dst_ref=rs2.at[d, :, aligned(c, pw)],
+    def inner3(c, d):
+        return pltpu.make_async_remote_copy(
+            src_ref=fin.at[:, mate(d), :, aligned(c, pw)],
+            dst_ref=in3.at[d, :, :, aligned(c, pw)],
             send_sem=send3.at[c, d],
             recv_sem=recv3.at[c, d],
-            device_id=(peer, band),
-            device_id_type=MESH,
-        )
+            **reach(z, mate(d)),
+        )
+
+    def outer3(c, e):
+        return pltpu.make_async_remote_copy(
+            src_ref=mid3.at[far(e), :, aligned(c, pw)],
+            dst_ref=end3.at[e, :, aligned(c, pw)],
+            send_sem=send3b.at[c, e],
+            recv_sem=recv3b.at[c, e],
+            **reach(far(e), w),
+        )
+
+    def middle3(c):
+        for d in range(1, inner):
+            inner3(c, d).wait()
+        for to in range(outer):
+            total = fin[to, w, :, aligned(c, pw)]
+            for d in range(1, inner):
+                total += in3[d, to, :, aligned(c, pw)]
+            mid3[to, :, aligned(c, pw)] = total
+        for e in range(1, outer):
+            outer3(c, e).start()
 
     for c in range(psi_chunks):
         psi_copy(c).wait()
 
-    def share(c, _):
+    def share(c):
         f = jnp.dot(s_buf[...], psi_v[:, aligned(c, pw)], preferred_element_type=F32)
         for b in range(2):
             at = 2 * b * cols
-            fin[b * cols : (b + 1) * cols, aligned(c, pw)] = (
-                f[at : at + cols] + f[at + cols : at + 2 * cols]
+            whole = f[at : at + cols] + f[at + cols : at + 2 * cols]
+            fin[b * half : (b + 1) * half, :, :, aligned(c, pw)] = whole.reshape(
+                half, inner, r2, pw
             )
-
-        def start3(d, _):
-            scatter3(c, d).start()
-            return 0
-
-        lax.fori_loop(1, n, start3, 0)
-        return 0
-
-    lax.fori_loop(0, psi_chunks, share, 0)
-
-    def finish(c, _):
-        def wait3(d, total):
-            scatter3(c, d).wait()
-            return total + rs2[d, :, aligned(c, pw)]
-
-        out_ref[:, aligned(c, pw)] = lax.fori_loop(
-            1, n, wait3, fin[aligned(me, r2), aligned(c, pw)]
-        )
-        return 0
-
-    lax.fori_loop(0, psi_chunks, finish, 0)
-
-
-def fused(n, blk, psi, trial, beta, q_blocks, atom_counts):
+        for d in range(1, inner):
+            inner3(c, d).start()
+
+    half = outer // 2
+    for c in range(psi_chunks):
+        share(c)
+        if c:
+            middle3(c - 1)
+    middle3(psi_chunks - 1)
+
+    for c in range(psi_chunks):
+        total = mid3[z, :, aligned(c, pw)]
+        for e in range(1, outer):
+            outer3(c, e).wait()
+            total += end3[e, :, aligned(c, pw)]
+        out_ref[:, aligned(c, pw)] = total
+
+
+def fused(n, inner, blk, psi, trial, beta, q_blocks, atom_counts):
     g, cols = trial.shape
     nbands = psi.shape[1]
     p_size = beta.shape[1]
@@ -270,12 +314,13 @@
     mp = -(-maxp // 8) * 8
     nd = -(-(2 * maxp - 1) // 8) * 8
     r1, r2 = cols // n, blk // n
+    outer = n // inner
     beta_chunks, psi_chunks, s_chunks = 3, 4, 8
     q_flat = jnp.pad(q_blocks, ((0, 0), (0, 0), (0, mp - maxp)))
     q_flat = q_flat.transpose(1, 2, 0).reshape(maxp * mp, natom)
     dma = pltpu.SemaphoreType.DMA
     out = pl.pallas_call(
-        functools.partial(kernel, n, maxp),
+        functools.partial(kernel, n, inner, maxp),
         out_shape=jax.ShapeDtypeStruct((r2, nbands), F32),
         in_specs=[pl.BlockSpec(memory_space=pl.ANY)] * 3
         + [pl.BlockSpec(memory_space=pltpu.VMEM)] * 2,
@@ -288,23 +333,33 @@
             pltpu.VMEM((3, maxp * mp, natom), BF16),
             pltpu.VMEM((nd, p_size), F32),
             pltpu.VMEM((cols, p_size), F32),
-            pltpu.VMEM((n, r1, p_size), F32),
+            pltpu.VMEM((inner, outer * r1, p_size), F32),
+            pltpu.VMEM((outer * r1, p_size), F32),
+            pltpu.VMEM((outer, r1, p_size), F32),
             pltpu.VMEM((cols, p_size), F32),
             pltpu.VMEM((2 * cols, p_size), BF16),
             pltpu.VMEM((4 * cols, g), BF16),
-            pltpu.VMEM((2 * cols, nbands), F32),
-            pltpu.VMEM((n, r2, nbands), F32),
+            pltpu.VMEM((outer, inner, r2, nbands), F32),
+            pltpu.VMEM((inner, outer, r2, nbands), F32),
+            pltpu.VMEM((outer, r2, nbands), F32),
+            pltpu.VMEM((outer, r2, nbands), F32),
             dma,
             dma((beta_chunks,)),
             dma((psi_chunks,)),
-            dma((beta_chunks, n)),
-            dma((beta_chunks, n)),
-            dma((n,)),
-            dma((n,)),
+            dma((beta_chunks, inner)),
+            dma((beta_chunks, inner)),
+            dma((beta_chunks, outer)),
+            dma((beta_chunks, outer)),
+            dma((outer,)),
+            dma((outer,)),
+            dma((outer, inner)),
+            dma((outer, inner)),
             dma((s_chunks,)),
             dma((s_chunks,)),
-            dma((psi_chunks, n)),
-            dma((psi_chunks, n)),
+            dma((psi_chunks, inner)),
+            dma((psi_chunks, inner)),
+            dma((psi_chunks, outer)),
+            dma((psi_chunks, outer)),
         ],
         compiler_params=pltpu.CompilerParams(
             collective_id=0, has_side_effects=True, vmem_limit_bytes=60 * 1024 * 1024
@@ -341,12 +396,14 @@
 
 def solution(mesh):
     n, bands = mesh.shape["ga"], mesh.shape["band"]
+    inner = 4
 
     def shards(psi, trial, beta, q_blocks, atom_counts):
         g, cols = trial.shape
         blk = cols * bands
         fits = (
             bands == 2
+            and n % (2 * inner) == 0
             and cols % 128 == 0
             and cols % (8 * n) == 0
             and blk % (8 * n) == 0
@@ -356,7 +413,7 @@
             and q_blocks.shape[0] % 128 == 0
         )
         if fits:
-            return fused(n, blk, psi, trial, beta, q_blocks, atom_counts)
+            return fused(n, inner, blk, psi, trial, beta, q_blocks, atom_counts)
         return general(psi, trial, beta, q_blocks, atom_counts)
 
     in_specs = (P("ga", "band"), P("ga", "band"), P("ga", None), P(), P())

time: 84.8 us -> 68.5 us (0.81)
  Pallas kernels: 81.5 us -> 65.2 us
    pallas_call x1, Pallas kernels: 81.5 us -> 65.2 us  [fused(): pl.pallas_call(functools.partial(kernel, n, inner, maxp), out_shape=jax.S...]
where the time goes in v2:
time: 68.5 us; the launch traced here: 68.3 us
  Pallas kernels  65.2 us (95%)
  local copies, waits for them, and re-layouts  3.1 us (5%)
    pallas_call x1, Pallas kernels, fused(): pl.pallas_call(functools.partial(kernel, n, inner, maxp), out_shape=jax.S...  65.2 us
    pad x1, local copies, waits for them, and re-layouts, fused(): q_flat = jnp.pad(q_blocks, ((0, 0), (0, 0), (0, mp - maxp)))  1.62 us
    unnamed x1, local copies, waits for them, and re-layouts  1.47 us

profile of v2, /device:TPU:0, one launch (start us, length us, event | category | flops | bytes accessed | tf_op | source)
XLA Modules:
  0.0 68.3 jit_solution(14598278654948082579)
XLA Ops:
  0.0 1.6 %pad.4 = f32[128,18,24]{0,2,1:T(8,128)} pad(f32[128,18,18]{0,2,1:T(8,128)} %param.8, f32[]{:T(128)} %constant.2.clone.1), padding=0_0x0_0x0_6 | pad | bytes 387076 | tf_op jit(solution)/shard_map/jit(_pad)/pad | solution.py:319
  1.6 65.2 %shard_map.55 = f32[16,1024]{1,0:T(8,128)} custom-call(bf16[4096,1024]{1,0:T(8,128)(2,1)} %psi_h.1, bf16[4096,128]{1,0:T(8,128)(2,1)} %trial_h.1, bf16[4096,1536]{1,0:T(8,128)(2,1)} %beta_h.1, f32[432,128]{1,0:T(8,128)} %bitcast.5, s32[1,128]{1,0:T(1,128)} %bitcast.7), custom_call_target="tpu_custom_call" | custom-call | tf_op jit(solution)/shard_map/pallas_call | solution.py:322
  66.8 1.5 %copy.7 = f32[1024,16]{0,1:T(8,128)} copy(f32[1024,16]{0,1:T(8,128)} %bitcast.6) | data formatting | bytes 131072

commit v3 on v2

--- a/solution.py
+++ b/solution.py
@@ -34,8 +34,11 @@
     outer = n // inner
     w, z = lax.rem(me, inner), lax.div(me, inner)
 
-    def mate(d):
-        return lax.rem(w + d, inner)
+    flip, cross = w + 1 - 2 * lax.rem(w, 2), lax.rem(w + 2, 4)
+    via = (1 - band) * flip + band * cross
+    last = band * flip + (1 - band) * cross
+    hop = {1: via, 2: last, 3: via}
+    meant = {1: via, 2: last, 3: 3 - w}
 
     def far(e):
         return lax.rem(z + e, outer)
@@ -77,8 +80,8 @@
 
     barrier = pltpu.get_barrier_semaphore()
 
-    for d in range(1, inner):
-        pl.semaphore_signal(barrier, inc=1, **reach(z, mate(d)))
+    for d in range(2):
+        pl.semaphore_signal(barrier, inc=1, **reach(z, (via, last)[d]))
     for e in range(1, outer):
         pl.semaphore_signal(barrier, inc=1, **reach(far(e), w))
     pl.semaphore_signal(barrier, inc=1, device_id=(me, 1 - band), device_id_type=MESH)
@@ -127,16 +130,16 @@
 
     lax.fori_loop(0, s_chunks, turn, 0)
 
-    pl.semaphore_wait(barrier, inner + outer - 1)
+    pl.semaphore_wait(barrier, outer + 2)
 
     def inner1(c, d):
         at = pl.ds(c * bw, bw)
         return pltpu.make_async_remote_copy(
-            src_ref=proj.at[aligned(mate(d), outer * r1), at],
+            src_ref=proj.at[aligned(meant[d], outer * r1), at],
             dst_ref=in1.at[d, :, at],
             send_sem=send1.at[c, d],
             recv_sem=recv1.at[c, d],
-            **reach(z, mate(d)),
+            **reach(z, hop[d]),
         )
 
     def outer1(c, e):
@@ -149,10 +152,16 @@
             **reach(far(e), w),
         )
 
+    def relay1(c):
+        at = pl.ds(c * bw, bw)
+        inner1(c, 3).wait()
+        proj[aligned(last, outer * r1), at] += in1[3, :, at]
+        inner1(c, 2).start()
+
     def middle1(c):
         at = pl.ds(c * bw, bw)
         total = proj[aligned(w, outer * r1), at]
-        for d in range(1, inner):
+        for d in (1, 2):
             inner1(c, d).wait()
             total += in1[d, :, at]
         mid1[:, at] = total
@@ -163,10 +172,14 @@
         beta_copy(c).wait()
         at = pl.ds(c * bw, bw)
         proj[:, at] = jnp.dot(trial_t[...], beta_v[:, at], preferred_element_type=F32)
-        for d in range(1, inner):
-            inner1(c, d).start()
-        if c:
-            middle1(c - 1)
+        inner1(c, 3).start()
+        inner1(c, 1).start()
+        if c > 0:
+            relay1(c - 1)
+        if c > 1:
+            middle1(c - 2)
+    relay1(beta_chunks - 1)
+    middle1(beta_chunks - 2)
     middle1(beta_chunks - 1)
 
     for c in range(beta_chunks):
@@ -193,13 +206,13 @@
         )
 
     def inner2(e, d):
-        block = w * outer + lax.rem(z + outer - e, outer)
+        block = (via if d == 3 else w) * outer + lax.rem(z + outer - e, outer)
         return pltpu.make_async_remote_copy(
             src_ref=wall.at[aligned(block, r1), :],
             dst_ref=wall.at[aligned(block, r1), :],
             send_sem=send2b.at[e, d],
             recv_sem=recv2b.at[e, d],
-            **reach(z, mate(d)),
+            **reach(z, via if d == 1 else last),
         )
 
     for e in range(1, outer):
@@ -207,10 +220,15 @@
     for e in range(outer):
         if e:
             outer2(e).wait()
-        for d in range(1, inner):
+        for d in (1, 2):
             inner2(e, d).start()
+        if e:
+            inner2(e - 1, 1).wait()
+            inner2(e - 1, 3).start()
+    inner2(outer - 1, 1).wait()
+    inner2(outer - 1, 3).start()
     for e in range(outer):
-        for d in range(1, inner):
+        for d in (2, 3):
             inner2(e, d).wait()
     hi, lo = split2(wall[...])
     whl[:cols, :] = hi
@@ -250,11 +268,11 @@
 
     def inner3(c, d):
         return pltpu.make_async_remote_copy(
-            src_ref=fin.at[:, mate(d), :, aligned(c, pw)],
+            src_ref=fin.at[:, meant[d], :, aligned(c, pw)],
             dst_ref=in3.at[d, :, :, aligned(c, pw)],
             send_sem=send3.at[c, d],
             recv_sem=recv3.at[c, d],
-            **reach(z, mate(d)),
+            **reach(z, hop[d]),
         )
 
     def outer3(c, e):
@@ -266,12 +284,18 @@
             **reach(far(e), w),
         )
 
+    def relay3(c):
+        inner3(c, 3).wait()
+        for to in range(outer):
+            fin[to, last, :, aligned(c, pw)] += in3[3, to, :, aligned(c, pw)]
+        inner3(c, 2).start()
+
     def middle3(c):
-        for d in range(1, inner):
+        for d in (1, 2):
             inner3(c, d).wait()
         for to in range(outer):
             total = fin[to, w, :, aligned(c, pw)]
-            for d in range(1, inner):
+            for d in (1, 2):
                 total += in3[d, to, :, aligned(c, pw)]
             mid3[to, :, aligned(c, pw)] = total
         for e in range(1, outer):
@@ -288,14 +312,18 @@
             fin[b * half : (b + 1) * half, :, :, aligned(c, pw)] = whole.reshape(
                 half, inner, r2, pw
             )
-        for d in range(1, inner):
-            inner3(c, d).start()
+        inner3(c, 3).start()
+        inner3(c, 1).start()
 
     half = outer // 2
     for c in range(psi_chunks):
         share(c)
-        if c:
-            middle3(c - 1)
+        if c > 0:
+            relay3(c - 1)
+        if c > 1:
+            middle3(c - 2)
+    relay3(psi_chunks - 1)
+    middle3(psi_chunks - 2)
     middle3(psi_chunks - 1)
 
     for c in range(psi_chunks):

time: 68.5 us -> 72.4 us (1.057)
  Pallas kernels: 65.2 us -> 69.1 us
    pallas_call x1, Pallas kernels: 65.2 us -> 69.1 us  [fused(): pl.pallas_call(functools.partial(kernel, n, inner, maxp), out_shape=jax.S...]
where the time goes in v3:
time: 72.4 us; the launch traced here: 72.2 us
  Pallas kernels  69.1 us (95%)
  local copies, waits for them, and re-layouts  3.1 us (4%)
    pallas_call x1, Pallas kernels, fused(): pl.pallas_call(functools.partial(kernel, n, inner, maxp), out_shape=jax.S...  69.1 us
    pad x1, local copies, waits for them, and re-layouts, fused(): q_flat = jnp.pad(q_blocks, ((0, 0), (0, 0), (0, mp - maxp)))  1.62 us
    unnamed x1, local copies, waits for them, and re-layouts  1.47 us

profile of v3, /device:TPU:0, one launch (start us, length us, event | category | flops | bytes accessed | tf_op | source)
XLA Modules:
  0.0 72.2 jit_solution(1858443727400314365)
XLA Ops:
  0.0 1.6 %pad.4 = f32[128,18,24]{0,2,1:T(8,128)} pad(f32[128,18,18]{0,2,1:T(8,128)} %param.8, f32[]{:T(128)} %constant.2.clone.1), padding=0_0x0_0x0_6 | pad | bytes 387076 | tf_op jit(solution)/shard_map/jit(_pad)/pad | solution.py:347
  1.6 69.1 %shard_map.55 = f32[16,1024]{1,0:T(8,128)} custom-call(bf16[4096,1024]{1,0:T(8,128)(2,1)} %psi_h.1, bf16[4096,128]{1,0:T(8,128)(2,1)} %trial_h.1, bf16[4096,1536]{1,0:T(8,128)(2,1)} %beta_h.1, f32[432,128]{1,0:T(8,128)} %bitcast.5, s32[1,128]{1,0:T(1,128)} %bitcast.7), custom_call_target="tpu_custom_call" | custom-call | tf_op jit(solution)/shard_map/pallas_call | solution.py:350
  70.7 1.5 %copy.7 = f32[1024,16]{0,1:T(8,128)} copy(f32[1024,16]{0,1:T(8,128)} %bitcast.6) | data formatting | bytes 131072
